TPU v7x, 32 devices: a 4x2x2 block of a 4x4x8 slice. The times are simulated.
32 devices in a mesh: dp: 4 (over y, z), tp: 8 (over x, core).
Axes of the slice: x: 4, y: 2, z: 2, core: 2. Of those that a mesh axis runs over, the one named last changes fastest.
The devices are a block of a 4x4x8 slice.
Arguments:
- x: bfloat16 [4, 2048, 4096], P('dp', 'tp'), parts along dimension 0
- ln_gain: bfloat16 [2, 4096], replicated
- ln_bias: bfloat16 [2, 4096], replicated
- w_q: bfloat16 [2, 4096, 16, 256], P(None, None, 'tp')
- b_q: bfloat16 [2, 16, 256], P(None, 'tp')
- w_k: bfloat16 [2, 4096, 16, 256], P(None, None, 'tp')
- b_k: bfloat16 [2, 16, 256], P(None, 'tp')
- w_v: bfloat16 [2, 4096, 16, 256], P(None, None, 'tp')
- b_v: bfloat16 [2, 16, 256], P(None, 'tp')
- w_o: bfloat16 [2, 16, 256, 4096], P(None, 'tp')
- b_o: bfloat16 [2, 4096], replicated
- w_up: bfloat16 [2, 4096, 16384], P(None, None, 'tp')
- b_up: bfloat16 [2, 16384], P(None, 'tp')
- w_down: bfloat16 [2, 16384, 4096], P(None, 'tp')
- b_down: bfloat16 [2, 4096], replicated
Outputs:
- output: bfloat16 [4, 2048, 4096], P('dp', 'tp'), parts along dimension 0
There are 4 independent parts. A program takes and returns all parts, laid end to end along the dimension named above; an argument that names none is the same for every part.
All inputs are finite; a program needn't handle non-finite values.
Results may differ from a plain program's by a relative error of at most 0.0171331.
Values are sent between devices in bfloat16 or wider.
A program may use at most 768 MiB of HBM per device.

v0:
```python
import jax
import jax.numpy as jnp
from jax import lax
from jax.sharding import PartitionSpec as P

ROT_DIM = 32
ROPE_BASE = 10000.0
LN_EPS = 1e-5


def rotary_tables(seq_len):
    half = ROT_DIM // 2
    inv_freq = 1.0 / (ROPE_BASE ** (jnp.arange(half, dtype=jnp.float32) * (2.0 / ROT_DIM)))
    angles = jnp.arange(seq_len, dtype=jnp.float32)[:, None] * inv_freq[None, :]
    return jnp.cos(angles), jnp.sin(angles)


def apply_rotary(projected, cosine, sine):
    half = ROT_DIM // 2
    first = projected[..., :half]
    second = projected[..., half:ROT_DIM]
    return jnp.concatenate([first * cosine - second * sine, second * cosine + first * sine, projected[..., ROT_DIM:]], axis=-1)


def layer_norm(hidden, gain, bias):
    x_f32 = hidden.astype(jnp.float32)
    mean = jnp.mean(x_f32, axis=-1, keepdims=True)
    centered = x_f32 - mean
    variance = jnp.mean(centered * centered, axis=-1, keepdims=True)
    return (centered * lax.rsqrt(variance + LN_EPS) * gain.astype(jnp.float32) + bias.astype(jnp.float32)).astype(jnp.bfloat16)


def causal_attention(q_rot, k_rot, values):
    seq_len = q_rot.shape[2]
    head_dim = q_rot.shape[3]
    scores = jnp.einsum("bhqe,bhke->bhqk", q_rot, k_rot, preferred_element_type=jnp.float32) * (head_dim ** -0.5)
    causal = jnp.arange(seq_len)[:, None] >= jnp.arange(seq_len)[None, :]
    attn_probs = jax.nn.softmax(jnp.where(causal, scores, -1e30), axis=-1).astype(jnp.bfloat16)
    return jnp.einsum("bhqk,bhke->bhqe", attn_probs, values, preferred_element_type=jnp.float32).astype(jnp.bfloat16)


def branch_partials(normed, cosine, sine, w_q, b_q, w_k, b_k, w_v, b_v, w_o, w_up, b_up, w_down):
    def project(weight, bias):
        return jnp.einsum("bld,dhe->bhle", normed, weight, preferred_element_type=jnp.float32) + bias.astype(jnp.float32)[None, :, None, :]

    q_rot = apply_rotary(project(w_q, b_q), cosine, sine).astype(jnp.bfloat16)
    k_rot = apply_rotary(project(w_k, b_k), cosine, sine).astype(jnp.bfloat16)
    values = project(w_v, b_v).astype(jnp.bfloat16)
    attended = causal_attention(q_rot, k_rot, values)
    up_act = jax.nn.gelu(jnp.einsum("bld,df->blf", normed, w_up, preferred_element_type=jnp.float32) + b_up.astype(jnp.float32), approximate=True).astype(jnp.bfloat16)
    return (jnp.einsum("bhle,hed->bld", attended, w_o, preferred_element_type=jnp.float32)
            + jnp.einsum("blf,fd->bld", up_act, w_down, preferred_element_type=jnp.float32))


def solution(mesh):
    tp_size = mesh.shape["tp"]
    head_spec = P(None, None, "tp", None)
    head_bias_spec = P(None, "tp", None)
    in_specs = (P("dp", "tp", None), P(), P(), head_spec, head_bias_spec, head_spec, head_bias_spec, head_spec, head_bias_spec,
                P(None, "tp", None, None), P(), P(None, None, "tp"), P(None, "tp"), P(None, "tp", None), P())

    def local_program(x_loc, ln_gain, ln_bias, w_q, b_q, w_k, b_k, w_v, b_v, w_o, b_o, w_up, b_up, w_down, b_down):
        cosine, sine = rotary_tables(x_loc.shape[1] * tp_size)
        hidden = x_loc
        for layer in range(w_q.shape[0]):
            normed = layer_norm(hidden, ln_gain[layer], ln_bias[layer])
            gathered = lax.all_gather(normed, "tp", axis=1, tiled=True)
            part_sum = branch_partials(gathered, cosine, sine, w_q[layer], b_q[layer], w_k[layer], b_k[layer], w_v[layer], b_v[layer],
                                       w_o[layer], w_up[layer], b_up[layer], w_down[layer]).astype(jnp.bfloat16)
            returned = lax.psum_scatter(part_sum, "tp", scatter_dimension=1, tiled=True)
            hidden = (hidden.astype(jnp.float32) + returned.astype(jnp.float32) + b_o[layer].astype(jnp.float32)
                      + b_down[layer].astype(jnp.float32)).astype(jnp.bfloat16)
        return hidden

    return jax.shard_map(local_program, mesh=mesh, in_specs=in_specs, out_specs=P("dp", "tp", None), check_vma=False)
```

profile of v0, /device:TPU:81, one launch (start us, length us, event | category | flops | bytes accessed | tf_op | source)
XLA Modules:
  0.0 738.2 jit_solution(7645032185660365327)
XLA Ops:
  6.6 1.5 slice_convert_fusion.7
  8.1 1.4 slice_convert_fusion.6
  9.5 2.0 convert_reduce_fusion.1
  11.4 2.3 fusion.80
  13.7 2.3 fusion.83
  16.4 8.5 %fusion.176 = (bf16[1,4096,2,256]{3,2,1,0:T(2,128)(2,1)}, bf16[1,4096,2,256]{3,2,1,0:T(2,128)(2,1)}) fusion(bf16[2,4096,2,256]{3,2,1,0:T(2,128)(2,1)} %param.20), kind=kLoop, calls=%fused_computation.202 | loop fusion | bytes 16777216 | tf_op jit(solution)/shard_map/slice | solution.py:68
  24.9 11.2 %copy.31 = bf16[1,4096,2,256]{1,3,2,0:T(8,128)(2,1)} copy(bf16[1,4096,2,256]{3,2,1,0:T(2,128)(2,1)} %get-tuple-element.10) | data formatting | bytes 8388608
  36.1 8.4 %fusion.175 = (bf16[1,4096,2,256]{3,2,1,0:T(2,128)(2,1)}, bf16[1,4096,2,256]{3,2,1,0:T(2,128)(2,1)}) fusion(bf16[2,4096,2,256]{3,2,1,0:T(2,128)(2,1)} %param.18), kind=kLoop, calls=%fused_computation.201 | loop fusion | bytes 16777216 | tf_op jit(solution)/shard_map/slice | solution.py:68
  44.5 11.2 %copy.30 = bf16[1,4096,2,256]{1,3,2,0:T(8,128)(2,1)} copy(bf16[1,4096,2,256]{3,2,1,0:T(2,128)(2,1)} %get-tuple-element.8) | data formatting | bytes 8388608
  55.8 0.6 bitcast_convert_fusion.1
  56.4 0.6 bitcast_convert_fusion.2
  57.0 0.6 bitcast_convert_fusion
  57.6 0.6 slice_convert_fusion.12
  58.2 0.5 fusion.153
  58.8 4.1 iota_compare_fusion
  62.9 8.5 %fusion.177 = (bf16[1,4096,2,256]{3,2,1,0:T(2,128)(2,1)}, bf16[1,4096,2,256]{3,2,1,0:T(2,128)(2,1)}) fusion(bf16[2,4096,2,256]{3,2,1,0:T(2,128)(2,1)} %param.22), kind=kLoop, calls=%fused_computation.203 | loop fusion | bytes 16777216 | tf_op jit(solution)/shard_map/slice | solution.py:68
  71.3 31.6 %all-gather.3.cloned.1.call-done = bf16[1,2048,4096]{2,1,0:T(8,128)(2,1)} async-done(((bf16[1,256,4096]{2,1,0:T(8,128)(2,1)}), bf16[1,2048,4096]{2,1,0:T(8,128)(2,1)}) %all-gather.3.cloned.1.call-update) | async-done | bytes 16777232 | tf_op jit(solution)/shard_map/all_gather | solution.py:67
  102.9 13.1 %fusion.94 = f32[1,2,2048,256]{2,3,1,0:T(8,128)S(1)} fusion(bf16[1,4096,2,256]{1,3,2,0:T(8,128)(2,1)} %copy.31, bf16[1,2048,4096]{2,1,0:T(8,128)(2,1)} %all-gather.3.cloned.1.call-done, f32[2,256]{1,0:T(2,128)S(1)} %get-tuple-element.38), kind=kOutput, calls=%fused_computation.112 | convolution fusion | flops 8590983168 | bytes 25167872 | tf_op jit(solution)/shard_map/bld,dhe->bhle/dot_general | solution.py:44
  116.0 11.7 %fusion.95 = f32[1,2,2048,256]{2,3,1,0:T(8,128)S(1)} fusion(bf16[1,4096,2,256]{1,3,2,0:T(8,128)(2,1)S(1)} %copy-done.4, bf16[1,2048,4096]{2,1,0:T(8,128)(2,1)} %all-gather.3.cloned.1.call-done, f32[2,256]{1,0:T(2,128)S(1)} %get-tuple-element.36), kind=kOutput, calls=%fused_computation.114 | convolution fusion | flops 8590983168 | bytes 25167872 | tf_op jit(solution)/shard_map/bld,dhe->bhle/dot_general | solution.py:44
  127.7 1.8 fusion.138
  129.7 19.7 %fusion.178 = (f32[2,2048]{1,0:T(2,128)S(1)}, f32[2,2048,2048]{1,2,0:T(8,128)}) fusion(pred[2048,2048]{0,1:T(8,128)(4,1)} %iota_compare_fusion, bf16[2,2048,224]{1,2,0:T(8,128)(2,1)} %get-tuple-element.48, bf16[2,2048,16]{1,2,0:T(8,128)(2,1)S(1)} %get-tuple-element.23, bf16[2,2048,16]{1,2,0:T(8,128)(2,1)S(1)} %get-tuple-element.24, ...), kind=kOutput, calls=%fused_computation.204 | convolution fusion | flops 4341106688 | bytes 41959424 | tf_op jit(solution)/shard_map/sub | solution.py:38
  149.4 13.6 %fusion.132 = bf16[2,2048,256]{2,1,0:T(8,128)(2,1)S(1)} fusion(bf16[1,4096,2,256]{3,2,1,0:T(2,128)(2,1)} %get-tuple-element.12, bf16[1,2048,4096]{2,1,0:T(8,128)(2,1)} %all-gather.3.cloned.1.call-done, f32[2,256]{1,0:T(2,128)S(1)} %get-tuple-element.40), kind=kOutput, calls=%fused_computation.133 | convolution fusion | flops 8592031744 | bytes 23070720 | tf_op jit(solution)/shard_map/bld,dhe->bhle/dot_general | solution.py:44
  163.0 27.9 %fusion.100 = f32[2048,4096,1]{1,0,2:T(8,128)} fusion(bf16[2,2,256,4096]{3,2,1,0:T(8,128)(2,1)} %param.24, bf16[2,2048,256]{2,1,0:T(8,128)(2,1)S(1)} %fusion.132, f32[2,2048,2048]{1,2,0:T(8,128)} %get-tuple-element.44, f32[2,2048]{1,0:T(2,128)S(1)} %get-tuple-element.43), kind=kOutput, calls=%fused_computation.119 | convolution fusion | flops 12902727680 | bytes 73416704 | tf_op jit(solution)/shard_map/bhle,hed->bld/dot_general | solution.py:51
  190.9 43.4 %fusion.33 = f32[2048,2048]{1,0:T(8,128)} fusion(bf16[1,2048,4096]{2,1,0:T(8,128)(2,1)} %all-gather.3.cloned.1.call-done, bf16[2,4096,2048]{2,1,0:T(8,128)(2,1)} %param.26), kind=kOutput, calls=%fused_computation.43 | convolution fusion | flops 34359738368 | bytes 50331648 | tf_op jit(solution)/shard_map/bld,df->blf/dot_general | solution.py:50
  234.3 47.8 %fusion.54 = bf16[1,2048,4096]{2,1,0:T(8,128)(2,1)} fusion(bf16[2,2048,4096]{2,1,0:T(8,128)(2,1)} %param.28, f32[2048,4096,1]{1,0,2:T(8,128)} %fusion.100, f32[2048,2048]{1,0:T(8,128)} %fusion.33, f32[2048]{0:T(1024)S(1)} %bitcast.241), kind=kOutput, calls=%fused_computation.65 | convolution fusion | flops 34418458624 | bytes 83894272 | tf_op jit(solution)/shard_map/blf,fd->bld/dot_general | solution.py:52
  282.2 0.6 copy-done.14
  282.8 0.6 slice_convert_fusion.5
  283.4 0.6 slice_convert_fusion.4
  284.0 86.7 %reduce-scatter.3.cloned.1.call-done = bf16[1,256,4096]{2,1,0:T(8,128)(2,1)} async-done(((bf16[1,2048,4096]{2,1,0:T(8,128)(2,1)}), bf16[1,256,4096]{2,1,0:T(8,128)(2,1)}) %reduce-scatter.3.cloned.1.call-update) | async-done | bytes 2097168 | tf_op jit(solution)/shard_map/reduce_scatter | solution.py:70
  370.7 2.7 convert_reduce_fusion
  373.5 0.7 fusion.76
  374.2 0.6 copy-done
  374.8 2.4 fusion.79
  377.3 0.2 reduce-scatter.5.cloned.1.call-start
  377.5 11.2 %copy.33 = bf16[1,4096,2,256]{1,3,2,0:T(8,128)(2,1)} copy(bf16[1,4096,2,256]{3,2,1,0:T(2,128)(2,1)} %get-tuple-element.7) | data formatting | bytes 8388608
  388.8 11.2 %copy.34 = bf16[1,4096,2,256]{1,3,2,0:T(8,128)(2,1)} copy(bf16[1,4096,2,256]{3,2,1,0:T(2,128)(2,1)} %get-tuple-element.9) | data formatting | bytes 8388608
  400.0 60.1 %all-gather.5.cloned.1.call-done = bf16[1,2048,4096]{2,1,0:T(8,128)(2,1)} async-done(((bf16[1,256,4096]{2,1,0:T(8,128)(2,1)}), bf16[1,2048,4096]{2,1,0:T(8,128)(2,1)}) %all-gather.5.cloned.1.call-update) | async-done | bytes 16777232 | tf_op jit(solution)/shard_map/all_gather | solution.py:67
  460.0 13.1 %fusion.92 = f32[1,2,2048,256]{2,3,1,0:T(8,128)S(1)} fusion(bf16[1,4096,2,256]{1,3,2,0:T(8,128)(2,1)} %copy.33, bf16[1,2048,4096]{2,1,0:T(8,128)(2,1)} %all-gather.5.cloned.1.call-done, f32[2,256]{1,0:T(2,128)S(1)} %copy-done.24), kind=kOutput, calls=%fused_computation.108 | convolution fusion | flops 8590983168 | bytes 25167872 | tf_op jit(solution)/shard_map/bld,dhe->bhle/dot_general | solution.py:44
  473.1 0.3 fusion.140
  473.4 11.7 %fusion.91 = f32[1,2,2048,256]{2,3,1,0:T(8,128)S(1)} fusion(bf16[1,4096,2,256]{1,3,2,0:T(8,128)(2,1)S(1)} %copy-done.5, bf16[1,2048,4096]{2,1,0:T(8,128)(2,1)} %all-gather.5.cloned.1.call-done, f32[2,256]{1,0:T(2,128)S(1)} %copy-done.23), kind=kOutput, calls=%fused_computation.106 | convolution fusion | flops 8590983168 | bytes 25167872 | tf_op jit(solution)/shard_map/bld,dhe->bhle/dot_general | solution.py:44
  485.3 1.5 fusion.141
  486.8 19.5 %fusion.179 = (f32[2,2048]{1,0:T(2,128)S(1)}, f32[2,2048,2048]{1,2,0:T(8,128)}) fusion(pred[2048,2048]{0,1:T(8,128)(4,1)} %iota_compare_fusion, bf16[2,2048,224]{1,2,0:T(8,128)(2,1)} %fusion.141, bf16[2,2048,16]{1,2,0:T(8,128)(2,1)S(1)} %get-tuple-element.21, bf16[2,2048,16]{1,2,0:T(8,128)(2,1)S(1)} %get-tuple-element.22, ...), kind=kOutput, calls=%fused_computation.205 | convolution fusion | flops 4341106688 | bytes 41959424 | tf_op jit(solution)/shard_map/sub | solution.py:38
  506.3 13.6 %fusion.135 = bf16[2,2048,256]{2,1,0:T(8,128)(2,1)S(1)} fusion(bf16[1,4096,2,256]{3,2,1,0:T(2,128)(2,1)} %get-tuple-element.11, bf16[1,2048,4096]{2,1,0:T(8,128)(2,1)} %all-gather.5.cloned.1.call-done, f32[2,256]{1,0:T(2,128)S(1)} %copy-done.22), kind=kOutput, calls=%fused_computation.134 | convolution fusion | flops 8592031744 | bytes 23070720 | tf_op jit(solution)/shard_map/bld,dhe->bhle/dot_general | solution.py:44
  519.9 28.0 %fusion.96 = f32[2048,4096,1]{1,0,2:T(8,128)} fusion(bf16[2,2,256,4096]{3,2,1,0:T(8,128)(2,1)} %param.24, bf16[2,2048,256]{2,1,0:T(8,128)(2,1)S(1)} %fusion.135, f32[2,2048,2048]{1,2,0:T(8,128)} %get-tuple-element.46, f32[2,2048]{1,0:T(2,128)S(1)} %get-tuple-element.45), kind=kOutput, calls=%fused_computation.115 | convolution fusion | flops 12902727680 | bytes 73416704 | tf_op jit(solution)/shard_map/bhle,hed->bld/dot_general | solution.py:51
  548.0 42.9 %fusion.23 = f32[2048,2048]{1,0:T(8,128)} fusion(bf16[1,2048,4096]{2,1,0:T(8,128)(2,1)} %all-gather.5.cloned.1.call-done, bf16[2,4096,2048]{2,1,0:T(8,128)(2,1)} %param.26), kind=kOutput, calls=%fused_computation.33 | convolution fusion | flops 34359738368 | bytes 50331648 | tf_op jit(solution)/shard_map/bld,df->blf/dot_general | solution.py:50
  590.9 48.1 %fusion.57 = bf16[1,2048,4096]{2,1,0:T(8,128)(2,1)} fusion(bf16[2,2048,4096]{2,1,0:T(8,128)(2,1)} %param.28, f32[2048,4096,1]{1,0,2:T(8,128)} %fusion.96, f32[2048,2048]{1,0:T(8,128)} %fusion.23, f32[2048]{0:T(1024)S(1)} %bitcast.240), kind=kOutput, calls=%fused_computation.66 | convolution fusion | flops 34418458624 | bytes 83894272 | tf_op jit(solution)/shard_map/blf,fd->bld/dot_general | solution.py:52
  639.0 88.6 %reduce-scatter.5.cloned.1.call-done = bf16[1,256,4096]{2,1,0:T(8,128)(2,1)} async-done(((bf16[1,2048,4096]{2,1,0:T(8,128)(2,1)}), bf16[1,256,4096]{2,1,0:T(8,128)(2,1)}) %reduce-scatter.5.cloned.1.call-update) | async-done | bytes 2097168 | tf_op jit(solution)/shard_map/reduce_scatter | solution.py:70
  727.6 3.7 fusion.89
  (62 shorter events, 0.9 us)
Async XLA Ops:
  6.5 7.2 copy-start.2
  6.5 96.4 %all-gather.3.cloned.1.call-start = ((), (), s32[]{:S(2)}) async-start(), calls=%async_computation.2 | async-start | bytes 18874368 | tf_op jit(solution)/shard_map/all_gather | solution.py:67
  16.1 354.6 %reduce-scatter.3.cloned.1.call-start = ((), (), s32[]{:S(2)}) async-start(), calls=%async_computation.3 | async-start | bytes 18874368 | tf_op jit(solution)/shard_map/reduce_scatter | solution.py:70
  44.5 11.3 %copy-start.19 = (bf16[2,2,256]{2,1,0:T(2,128)(2,1)S(1)}, bf16[2,2,256]{2,1,0:T(2,128)(2,1)}, u32[]{:S(2)}) copy-start(bf16[2,2,256]{2,1,0:T(2,128)(2,1)} %param.21) | copy-start | bytes 6148
  44.5 11.9 %copy-start.20 = (bf16[2,2,256]{2,1,0:T(2,128)(2,1)S(1)}, bf16[2,2,256]{2,1,0:T(2,128)(2,1)}, u32[]{:S(2)}) copy-start(bf16[2,2,256]{2,1,0:T(2,128)(2,1)} %param.19) | copy-start | bytes 6148
  44.5 12.5 %copy-start.21 = (bf16[2,2,256]{2,1,0:T(2,128)(2,1)S(1)}, bf16[2,2,256]{2,1,0:T(2,128)(2,1)}, u32[]{:S(2)}) copy-start(bf16[2,2,256]{2,1,0:T(2,128)(2,1)} %param.23) | copy-start | bytes 6148
  44.5 13.0 %copy-start.16 = (bf16[2,2048]{1,0:T(2,128)(2,1)S(1)}, bf16[2,2048]{1,0:T(2,128)(2,1)}, u32[]{:S(2)}) copy-start(bf16[2,2048]{1,0:T(2,128)(2,1)} %param.27) | copy-start | bytes 24580
  58.7 70.8 %copy-start.6 = (f32[2048,16]{0,1:T(8,128)}, f32[2048,16]{0,1:T(8,128)S(1)}, u32[]{:S(2)}) copy-start(f32[2048,16]{0,1:T(8,128)S(1)} %get-tuple-element.41) | copy-start | bytes 393220
  58.7 70.8 %copy-start.8 = (f32[2048,16]{0,1:T(8,128)}, f32[2048,16]{0,1:T(8,128)S(1)}, u32[]{:S(2)}) copy-start(f32[2048,16]{0,1:T(8,128)S(1)} %get-tuple-element.42) | copy-start | bytes 393220
  102.9 13.1 %copy-start.4 = (bf16[1,4096,2,256]{1,3,2,0:T(8,128)(2,1)S(1)}, bf16[1,4096,2,256]{1,3,2,0:T(8,128)(2,1)}, u32[]{:S(2)}) copy-start(bf16[1,4096,2,256]{1,3,2,0:T(8,128)(2,1)} %copy.30) | copy-start | bytes 12582916
  190.9 43.4 %copy-start.18 = (f32[1,2048]{1,0:T(1,128)S(1)}, f32[1,2048]{1,0:T(1,128)}, u32[]{:S(2)}) copy-start(f32[1,2048]{1,0:T(1,128)} %get-tuple-element.34) | copy-start | bytes 24580
  282.1 0.7 copy-start.14
  282.1 1.3 copy-start.15
  282.1 88.6 %copy-start.3 = (bf16[1,256,4096]{2,1,0:T(8,128)(2,1)S(1)}, bf16[1,256,4096]{2,1,0:T(8,128)(2,1)}, u32[]{:S(2)}) copy-start(bf16[1,256,4096]{2,1,0:T(8,128)(2,1)} %param.15) | copy-start | bytes 6291460
  282.1 177.9 %all-gather.5.cloned.1.call-start = ((), (), s32[]{:S(2)}) async-start(), calls=%async_computation.4 | async-start | bytes 18874368 | tf_op jit(solution)/shard_map/all_gather | solution.py:67
  370.7 4.1 copy-start.10
  370.7 4.1 copy-start.11
  373.5 1.3 copy-start
  377.3 350.4 %reduce-scatter.5.cloned.1.call-start = ((), (), s32[]{:S(2)}) async-start(), calls=%async_computation.5 | async-start | bytes 18874368 | tf_op jit(solution)/shard_map/reduce_scatter | solution.py:70
  388.8 71.3 %copy-start.24 = (f32[2,256]{1,0:T(2,128)S(1)}, f32[2,256]{1,0:T(2,128)}, u32[]{:S(2)}) copy-start(f32[2,256]{1,0:T(2,128)} %get-tuple-element.35) | copy-start | bytes 6148
  460.0 13.4 %copy-start.5 = (bf16[1,4096,2,256]{1,3,2,0:T(8,128)(2,1)S(1)}, bf16[1,4096,2,256]{1,3,2,0:T(8,128)(2,1)}, u32[]{:S(2)}) copy-start(bf16[1,4096,2,256]{1,3,2,0:T(8,128)(2,1)} %copy.34) | copy-start | bytes 12582916
  460.0 13.4 %copy-start.23 = (f32[2,256]{1,0:T(2,128)S(1)}, f32[2,256]{1,0:T(2,128)}, u32[]{:S(2)}) copy-start(f32[2,256]{1,0:T(2,128)} %get-tuple-element.37) | copy-start | bytes 6148
  473.4 11.8 %copy-start.7 = (f32[2048,16]{0,1:T(8,128)S(1)}, f32[2048,16]{0,1:T(8,128)}, u32[]{:S(2)}) copy-start(f32[2048,16]{0,1:T(8,128)} %copy-done.6) | copy-start | bytes 393220
  473.4 11.8 %copy-start.9 = (f32[2048,16]{0,1:T(8,128)S(1)}, f32[2048,16]{0,1:T(8,128)}, u32[]{:S(2)}) copy-start(f32[2048,16]{0,1:T(8,128)} %copy-done.8) | copy-start | bytes 393220
  486.8 19.5 %copy-start.22 = (f32[2,256]{1,0:T(2,128)S(1)}, f32[2,256]{1,0:T(2,128)}, u32[]{:S(2)}) copy-start(f32[2,256]{1,0:T(2,128)} %get-tuple-element.39) | copy-start | bytes 6148
  548.0 42.9 %copy-start.17 = (f32[1,2048]{1,0:T(1,128)S(1)}, f32[1,2048]{1,0:T(1,128)}, u32[]{:S(2)}) copy-start(f32[1,2048]{1,0:T(1,128)} %get-tuple-element.33) | copy-start | bytes 24580
  639.0 88.7 %copy-start.1 = (bf16[1,256,4096]{2,1,0:T(8,128)(2,1)S(1)}, bf16[1,256,4096]{2,1,0:T(8,128)(2,1)}, u32[]{:S(2)}) copy-start(bf16[1,256,4096]{2,1,0:T(8,128)(2,1)} %copy-done) | copy-start | bytes 6291460
  639.0 88.7 %copy-start.12 = (f32[1,4096]{1,0:T(1,128)S(1)}, f32[1,4096]{1,0:T(1,128)}, u32[]{:S(2)}) copy-start(f32[1,4096]{1,0:T(1,128)} %get-tuple-element.25) | copy-start | bytes 49156
  639.0 88.7 %copy-start.13 = (f32[1,4096]{1,0:T(1,128)S(1)}, f32[1,4096]{1,0:T(1,128)}, u32[]{:S(2)}) copy-start(f32[1,4096]{1,0:T(1,128)} %get-tuple-element.27) | copy-start | bytes 49156
Sparse Core Ops, SparseCore 0:
  16.3 86.6 all-gather.2
  282.3 88.4 reduce-scatter.2
  377.4 82.5 all-gather.4
  639.2 88.4 reduce-scatter.4
where the time goes:
time: 743 us; the launch traced here: 738 us
  matrix products  354 us (48%)
  waiting for transfers between devices  267 us (36%)
  local copies, waits for them, and re-layouts  75.1 us (10%)
  other arithmetic  27.6 us (4%)
  between operations  13.7 us (2%)
    reduce_scatter x2, waiting for transfers between devices, local_program(): returned = lax.psum_scatter(part_sum, 'tp', scatter_dimension=1, tiled=True)  175 us
    dot_general x2, matrix products, branch_partials(): jnp.einsum('blf,fd->bld', up_act, w_down, preferred_element_type=jnp.floa...  95.9 us
    all_gather x2, waiting for transfers between devices, local_program(): gathered = lax.all_gather(normed, 'tp', axis=1, tiled=True)  91.6 us
    dot_general x2, matrix products, branch_partials(): jnp.einsum('bld,df->blf', normed, w_up, preferred_element_type=jnp.float32)  86.3 us
    dot_general x6, matrix products, project(): jnp.einsum('bld,dhe->bhle', normed, weight, preferred_element_type=jnp.fl...  76.8 us
    dot_general x2, matrix products, branch_partials(): jnp.einsum('bhle,hed->bld', attended, w_o, preferred_element_type=jnp.flo...  55.9 us
    unnamed x54, local copies, waits for them, and re-layouts  46.2 us
    sub x2, matrix products, causal_attention(): jax.nn.softmax(jnp.where(causal, scores, -1e+30), axis=-1)  39.2 us
  transfers between devices with their start and end apart: 4, of which 4 were waited for; matrix products, arithmetic and copies ran while one was open for 11% of the time, Pallas kernels for 0%

commit v1 on v0

v1 whole, which is shorter than its diff:
```python
import functools

import jax
import jax.numpy as jnp
import numpy as np
from jax import lax
from jax.experimental import pallas as pl
from jax.experimental.pallas import tpu as pltpu
from jax.sharding import PartitionSpec as P

BF16, F32 = jnp.bfloat16, jnp.float32
MESH = pl.DeviceIdType.MESH
ROT_DIM, ROPE_BASE, LN_EPS = 32, 10000.0, 1e-5
CHIPS, GROUPS, R = 4, 4, 64
SUB = 2 * R
CHUNK = GROUPS * SUB
VMEM_LIMIT = 66_900_000


def rotary_constants(seq_len):
    inv_freq = 1.0 / ROPE_BASE ** (np.arange(ROT_DIM // 2) * (2.0 / ROT_DIM))

    def table(positions):
        angles = positions[:, None] * inv_freq[None, :]
        cos, sin = np.ones((len(positions), 128)), np.zeros((len(positions), 128))
        cos[:, :ROT_DIM] = np.concatenate([np.cos(angles), np.cos(angles)], axis=1)
        sin[:, :ROT_DIM] = np.concatenate([-np.sin(angles), np.sin(angles)], axis=1)
        return cos.astype(np.float32), sin.astype(np.float32)

    return table(np.arange(R, dtype=np.float64)) + table(np.arange(0, seq_len, R, dtype=np.float64))


def place():
    tp = lax.axis_index("tp")
    chip, core = tp // 2, tp % 2
    right = {"tp": ((chip + 1) % CHIPS) * 2 + core}
    left = {"tp": ((chip + CHIPS - 1) % CHIPS) * 2 + core}
    sibling = {"tp": chip * 2 + 1 - core}
    return chip, core, right, left, sibling


def greet(peers):
    barrier = pltpu.get_barrier_semaphore()
    for peer in peers:
        pl.semaphore_signal(barrier, inc=1, device_id=peer, device_id_type=MESH)
    pl.semaphore_wait(barrier, len(peers))


def rows_at(start, size):
    return pl.ds(pl.multiple_of(start, R), size)


def remote(src, dst, send, recv, peer):
    return pltpu.make_async_remote_copy(src_ref=src, dst_ref=dst, send_sem=send, recv_sem=recv, device_id=peer, device_id_type=MESH)


def gelu(x):
    inner = x * (0.7978845608028654 + (0.7978845608028654 * 0.044715) * (x * x))
    return x * (0.5 + 0.5 * jnp.tanh(inner))


def project_kernel(layer, x_ref, gain_ref, bias_ref, bq_ref, bk_ref, bv_ref, bup_ref, cosr_ref, sinr_ref, cosb_ref, sinb_ref,
                   wq_hbm, wk_hbm, wv_hbm, wup_hbm, y_hbm, h_buf, wqkv, wup, raw, out_buf,
                   near_send, near_recv, far_send, far_recv, sib_send, sib_recv, up_sem, raw_sem, out_sem):
    chip, core, right, left, sibling = place()
    depth, width = wup.shape
    head = wq_hbm.shape[3]
    qkv = 2 * head
    n_up = width // 512
    kstep = raw.shape[1]
    slots = raw.shape[0]
    per = depth // kstep
    total_raw = 3 * per

    def up_copy(n):
        cols = pl.ds(n * 512, 512)
        return pltpu.make_async_copy(wup_hbm.at[layer, :, cols], wup.at[:, cols], up_sem.at[n])

    def raw_copy(j):
        w = (wq_hbm, wk_hbm, wv_hbm)[j // per]
        return pltpu.make_async_copy(w.at[layer, pl.ds((j % per) * kstep, kstep)], raw.at[j % slots], raw_sem.at[j % slots])

    for j in range(slots):
        raw_copy(j).start()
    for n in range(n_up):
        up_copy(n).start()
    greet((right, left, sibling))

    def group(c, g, k):
        return h_buf.at[rows_at(c * CHUNK + g * SUB + k * R, R)]

    left_chip, right_chip, far_chip = (chip + CHIPS - 1) % CHIPS, (chip + 1) % CHIPS, (chip + 2) % CHIPS

    def near(side, g):
        blk = group(chip, g, core)
        return remote(blk, blk, near_send.at[side, g], near_recv.at[side, g], (right, left)[side])

    def near_in(side, g):
        blk = group((left_chip, right_chip)[side], g, core)
        return remote(blk, blk, near_send.at[side, g], near_recv.at[side, g], (right, left)[side])

    def far(side, b):
        blk = group((left_chip, right_chip)[side], side * 2 + b, core)
        return remote(blk, blk, far_send.at[side, b], far_recv.at[side, b], (right, left)[side])

    def far_in(side, b):
        blk = group(far_chip, side * 2 + b, core)
        return remote(blk, blk, far_send.at[side, b], far_recv.at[side, b], (right, left)[side])

    def share(slot, c, g, k):
        blk = group(c, g, k)
        return remote(blk, blk, sib_send.at[slot, g], sib_recv.at[slot, g], sibling)

    gain = gain_ref[layer:layer + 1, :].astype(F32)
    bias = bias_ref[layer:layer + 1, :].astype(F32)

    def normalize(g):
        def strip(j, carry):
            x = x_ref[pl.ds(pl.multiple_of(g * R + j * 16, 16), 16), :].astype(F32)
            mean = jnp.mean(x, axis=-1, keepdims=True)
            cen = x - mean
            var = jnp.mean(cen * cen, axis=-1, keepdims=True)
            out = (cen * lax.rsqrt(var + LN_EPS) * gain + bias).astype(BF16)
            h_buf[pl.ds(pl.multiple_of(chip * CHUNK + g * SUB + core * R + j * 16, 16), 16), :] = out
            return carry
        lax.fori_loop(0, R // 16, strip, 0)

    for g, side in ((0, 0), (2, 1), (1, 0), (3, 1)):
        normalize(g)
        near(side, g).start()
        share(0, chip, g, core).start()
    for g, side in ((2, 0), (0, 1), (3, 0), (1, 1)):
        near(side, g).start()

    for j in range(total_raw):
        raw_copy(j).wait()
        x = jnp.swapaxes(raw[j % slots], 0, 1)
        for hd in range(2):
            wqkv[pl.ds((j % per) * kstep, kstep), pl.ds((j // per) * qkv + hd * head, head)] = x[hd]
        if j + slots < total_raw:
            raw_copy(j + slots).start()
    for n in range(n_up):
        up_copy(n).wait()

    def exchange(b):
        for side in range(2):
            g = (b + 2 * side) % GROUPS
            near_in(side, g).wait_recv()
            share(1 + side, (left_chip, right_chip)[side], g, core).start()

            @pl.when(b < 2)
            def _():
                far(side, b).start()

    def exchange_far(b):
        for side in range(2):
            far_in(side, b).wait_recv()
            share(3, far_chip, side * 2 + b, core).start()

    lane = lax.broadcasted_iota(jnp.int32, (SUB, 128), 1)

    def out_copy(slot, row0):
        return pltpu.make_async_copy(out_buf.at[slot], y_hbm.at[rows_at(row0, SUB)], out_sem.at[slot])

    def coords(i):
        near_b, near_s = (i - 4) // 2, (i - 4) % 2
        far_b, far_s = (i - 12) // 2, (i - 12) % 2
        is_own, is_far = i < 4, i >= 12
        slot = jnp.where(is_own, 0, jnp.where(is_far, 3, 1 + near_s))
        c = (chip + jnp.where(is_own, 0, jnp.where(is_far, 2, jnp.where(near_s == 0, CHIPS - 1, 1)))) % CHIPS
        g = jnp.where(is_own, i, jnp.where(is_far, far_s * 2 + far_b, (near_b + 2 * near_s) % GROUPS))
        return slot, c, g

    def piece(i, carry):
        @pl.when(jnp.logical_and(jnp.logical_and(i >= 3, i <= 9), i % 2 == 1))
        def _():
            exchange((i - 3) // 2)

        @pl.when(i == 11)
        def _():
            exchange_far(0)

        @pl.when(i == 14)
        def _():
            exchange_far(1)

        slot, c, g = coords(i)
        share(slot, c, g, 1 - core).wait_recv()
        row0 = c * CHUNK + g * SUB
        rows = rows_at(row0, SUB)
        o = i % 2

        @pl.when(i >= 2)
        def _():
            _, c2, g2 = coords(i - 2)
            out_copy(o, c2 * CHUNK + g2 * SUB).wait()

        for n in range(n_up):
            cols = slice(n * 512, (n + 1) * 512)
            acc = jnp.dot(h_buf[rows, :], wup[:, cols], preferred_element_type=F32) + bup_ref[layer:layer + 1, cols].astype(F32)
            out_buf[o, :, 3 * qkv + n * 512:3 * qkv + (n + 1) * 512] = gelu(acc).astype(BF16)
        pos_blk = c * (CHUNK // R) + g
        for j, b_ref in enumerate((bq_ref, bk_ref, bv_ref)):
            acc = jnp.dot(h_buf[rows, :], wqkv[:, j * qkv:(j + 1) * qkv], preferred_element_type=F32)
            for hd in range(2):
                lo = j * qkv + hd * head
                val = acc[:, hd * head:(hd + 1) * head] + b_ref[layer, hd:hd + 1, :].astype(F32)
                if j == 2:
                    out_buf[o, :, lo:lo + head] = val.astype(BF16)
                    continue
                u = val[:, :128]
                partner = jnp.where(lane < ROT_DIM // 2, pltpu.roll(u, 128 - ROT_DIM // 2, 1), pltpu.roll(u, ROT_DIM // 2, 1))
                for k in range(2):
                    cb = cosb_ref[pl.ds(pos_blk + k * GROUPS, 1), :]
                    sb = sinb_ref[pl.ds(pos_blk + k * GROUPS, 1), :]
                    cos = cb * cosr_ref[...] - sb * sinr_ref[...]
                    sin = sb * cosr_ref[...] + cb * sinr_ref[...]
                    part = slice(k * R, (k + 1) * R)
                    out_buf[o, part, lo:lo + 128] = (u[part] * cos + partner[part] * sin).astype(BF16)
                out_buf[o, :, lo + 128:lo + head] = val[:, 128:].astype(BF16)
        out_copy(o, row0).start()
        return carry

    lax.fori_loop(0, 16, piece, 0)
    for i in (14, 15):
        _, c, g = coords(i)
        out_copy(i % 2, c * CHUNK + g * SUB).wait()
    for g in range(GROUPS):
        for side in range(2):
            near(side, g).wait_send()
        for slot in range(4):
            share(slot, (chip, left_chip, right_chip, far_chip)[slot], g, core).wait_send()
    for side in range(2):
        for b in range(2):
            far(side, b).wait_send()


def project(layer, x, ln_gain, ln_bias, w_q, b_q, w_k, b_k, w_v, b_v, w_up, b_up, tables):
    depth, width = w_up.shape[1:]
    seq = CHIPS * CHUNK
    qkv = 3 * w_q.shape[2] * w_q.shape[3]
    vmem, hbm = pl.BlockSpec(memory_space=pltpu.VMEM), pl.BlockSpec(memory_space=pltpu.HBM)
    dma = pltpu.SemaphoreType.DMA
    flops = 2 * seq * depth * (qkv + width)
    return pl.pallas_call(
        functools.partial(project_kernel, layer),
        out_shape=jax.ShapeDtypeStruct((seq, qkv + width), BF16),
        in_specs=[vmem] * 11 + [hbm] * 4,
        out_specs=hbm,
        scratch_shapes=[
            pltpu.VMEM((seq, depth), BF16), pltpu.VMEM((depth, qkv), BF16), pltpu.VMEM((depth, width), BF16),
            pltpu.VMEM((6, 512) + w_q.shape[2:], BF16), pltpu.VMEM((2, SUB, qkv + width), BF16),
            dma((2, 4)), dma((2, 4)), dma((2, 2)), dma((2, 2)), dma((4, 4)), dma((4, 4)), dma((width // 512,)), dma((6,)), dma((2,)),
        ],
        compiler_params=pltpu.CompilerParams(collective_id=2 * layer, has_side_effects=True, vmem_limit_bytes=VMEM_LIMIT),
        cost_estimate=pl.CostEstimate(flops=flops, bytes_accessed=60_000_000, transcendentals=seq * width),
        name=f"project_{layer}",
    )(x, ln_gain, ln_bias, b_q, b_k, b_v, b_up, *tables, w_q, w_k, w_v, w_up)


def combine_kernel(layer, x_ref, bo_ref, bd_ref, y_hbm, wo_hbm, wd_hbm, out_ref,
                   wo, wd, keys, vals, q_buf, a_buf, s_buf, o_buf, att, part, sib_in, far_in, fin_in, send_buf,
                   w_sem, q_sem, a_sem, sib_send, sib_recv, ici_send, far_recv, fin_recv):
    chip, core, right, left, sibling = place()
    qkv = wo.shape[0]
    head = qkv // 2
    inner, depth = wd.shape
    left_chip, right_chip, far_chip = (chip + CHIPS - 1) % CHIPS, (chip + 1) % CHIPS, (chip + 2) % CHIPS

    def where_is(i):
        s, b = i % 2, (i // 2) % 2
        stage = i // 4
        c = jnp.where(stage == 0, far_chip, jnp.where(stage == 3, chip, jnp.where(s == 0, right_chip, left_chip)))
        half = jnp.where(stage == 1, 1 - s, s)
        return c, half * 2 + b

    def row_of(i):
        c, g = where_is(i)
        return c * CHUNK + g * SUB

    def q_copy(i):
        return pltpu.make_async_copy(y_hbm.at[rows_at(row_of(i), SUB), pl.ds(0, qkv)], q_buf.at[i], q_sem.at[i])

    def a_copy(i):
        return pltpu.make_async_copy(y_hbm.at[rows_at(row_of(i), SUB), pl.ds(3 * qkv, inner)], a_buf.at[i], a_sem.at[i])

    loads = [pltpu.make_async_copy(y_hbm.at[:, pl.ds(qkv, qkv)], keys, w_sem.at[0]),
             pltpu.make_async_copy(y_hbm.at[:, pl.ds(2 * qkv, qkv)], vals, w_sem.at[1]),
             pltpu.make_async_copy(wo_hbm.at[layer], wo, w_sem.at[2])]
    wd_loads = [pltpu.make_async_copy(wd_hbm.at[layer, :, pl.ds(n * 1024, 1024)], wd.at[:, pl.ds(n * 1024, 1024)], w_sem.at[3 + n])
                for n in range(depth // 1024)]
    q_copy(0).start()
    a_copy(0).start()
    for cp in loads + wd_loads:
        cp.start()
    for i in range(1, 16):
        q_copy(i).start()
        a_copy(i).start()
    greet((right, left, sibling))

    scale = (head ** -0.5) * 1.4426950408889634
    krow = lax.broadcasted_iota(jnp.int32, (SUB, CHUNK), 1)
    kpos = (krow // R % 2) * (CHUNK // 2) + (krow // SUB) * R + krow % R
    qrow = lax.broadcasted_iota(jnp.int32, (SUB, CHUNK), 0)

    def lanes(x, op):
        r = x[:, 0:128]
        for j in range(1, x.shape[1] // 128):
            r = op(r, x[:, j * 128:(j + 1) * 128])
        return r

    def attend(i):
        t, g = where_is(i)
        qpos = (qrow // R) * (CHUNK // 2) + g * R + qrow % R

        def scores(kb, hd):
            return lax.dot_general(q_buf[i, :, hd * head:(hd + 1) * head], keys[rows_at(kb * CHUNK, CHUNK), hd * head:(hd + 1) * head],
                                   (((1,), (1,)), ((), ())), preferred_element_type=F32)

        top = []
        for hd in range(2):
            s = jnp.where(qpos >= kpos, scores(t, hd), -1e30)
            s_buf[hd, t] = s
            top.append(lanes(s, jnp.maximum))

        def first(kb, top):
            new = []
            for hd in range(2):
                s = scores(kb, hd)
                s_buf[hd, kb] = s
                new.append(jnp.maximum(top[hd], lanes(s, jnp.maximum)))
            return tuple(new)

        top = lax.fori_loop(0, t, first, tuple(top))
        top = [jnp.max(m, axis=1, keepdims=True) * scale for m in top]

        def second(kb, tot):
            new = []
            for hd in range(2):
                e = jnp.exp2(s_buf[hd, kb] * scale - top[hd])
                s_buf[hd, kb] = e
                new.append(tot[hd] + lanes(e, jnp.add))
            return tuple(new)

        zero = jnp.zeros((SUB, 128), F32)
        tot = lax.fori_loop(0, t + 1, second, (zero, zero))
        inv = [1.0 / jnp.sum(v, axis=1, keepdims=True) for v in tot]

        def weighted(kb, hd):
            p = (s_buf[hd, kb] * inv[hd]).astype(BF16)
            return jnp.dot(p, vals[rows_at(kb * CHUNK, CHUNK), hd * head:(hd + 1) * head], preferred_element_type=F32)

        for hd in range(2):
            o_buf[hd] = weighted(t, hd)

        def third(kb, carry):
            for hd in range(2):
                o_buf[hd] += weighted(kb, hd)
            return carry

        lax.fori_loop(0, t, third, 0)
        for hd in range(2):
            att[:, hd * head:(hd + 1) * head] = o_buf[hd].astype(BF16)

    def to_sibling(i):
        return remote(part.at[i % 2, rows_at((1 - core) * R, R)], sib_in.at[i % 4], sib_send.at[i % 2], sib_recv.at[i % 4], sibling)

    def out_far(i):
        s, b = i % 2, i // 2
        return [remote(send_buf.at[i], far_in.at[side, b], ici_send.at[i], far_recv.at[side, b], (right, left)[side]) for side in range(2)], s

    def out_fin(i):
        s = i % 2
        _, g = where_is(i)
        return [remote(send_buf.at[i], fin_in.at[side, g], ici_send.at[i], fin_recv.at[side, g], (right, left)[side]) for side in range(2)], s

    def start_by_side(pair):
        copies, s = pair
        for side in range(2):
            @pl.when(s == side)
            def _():
                copies[side].start()

    STRIP = 16

    def merge(i, extra):
        to_sibling(i).wait_recv()

        def strip(j, carry):
            r = pl.ds(pl.multiple_of(j * STRIP, STRIP), STRIP)
            v = part[i % 2, pl.ds(pl.multiple_of(core * R + j * STRIP, STRIP), STRIP), :].astype(F32) + sib_in[i % 4, r, :].astype(F32)
            if extra:
                v += far_in[i % 2, (i // 2) % 2, r, :].astype(F32)
            send_buf[i, r, :] = v.astype(BF16)
            return carry

        lax.fori_loop(0, R // STRIP, strip, 0)

    def settle(i):
        @pl.when(i < 4)
        def _():
            merge(i, False)
            start_by_side(out_far(i))

        @pl.when(jnp.logical_and(i >= 4, i < 8))
        def _():
            merge(i, False)
            start_by_side(out_fin(i))

        @pl.when(jnp.logical_and(i >= 8, i < 12))
        def _():
            s, b = i % 2, (i // 2) % 2
            for side in range(2):
                @pl.when(s == side)
                def _():
                    remote(send_buf.at[i], far_in.at[side, b], ici_send.at[i], far_recv.at[side, b], (right, left)[side]).wait_recv()
            merge(i, True)
            start_by_side(out_fin(i))

        @pl.when(i >= 12)
        def _():
            merge(i, False)

    def piece(i, carry):
        q_copy(i).wait()

        @pl.when(i == 0)
        def _():
            loads[0].wait()
            loads[1].wait()

        attend(i)
        a_copy(i).wait()

        @pl.when(i == 0)
        def _():
            loads[2].wait()
            for cp in wd_loads:
                cp.wait()

        @pl.when(i >= 2)
        def _():
            to_sibling(i - 2).wait_send()

        for n in range(depth // 512):
            cols = slice(n * 512, (n + 1) * 512)
            acc = (jnp.dot(a_buf[i], wd[:, cols], preferred_element_type=F32)
                   + jnp.dot(att[...], wo[:, cols], preferred_element_type=F32))
            part[i % 2, :, cols] = acc.astype(BF16)
        to_sibling(i).start()

        @pl.when(i >= 1)
        def _():
            settle(i - 1)

        return carry

    lax.fori_loop(0, 16, piece, 0)
    settle(15)
    for i in (14, 15):
        to_sibling(i).wait_send()

    both = bo_ref[layer:layer + 1, :].astype(F32) + bd_ref[layer:layer + 1, :].astype(F32)
    for i in range(12, 16):
        g = (i % 2) * 2 + (i // 2) % 2
        for side in range(2):
            remote(send_buf.at[i], fin_in.at[side, g], ici_send.at[0], fin_recv.at[side, g], (right, left)[side]).wait_recv()

        def strip(j, carry):
            r = pl.ds(pl.multiple_of(j * STRIP, STRIP), STRIP)
            xr = pl.ds(pl.multiple_of(g * R + j * STRIP, STRIP), STRIP)
            v = x_ref[xr, :].astype(F32) + send_buf[i, r, :].astype(F32)
            v = v + fin_in[0, g, r, :].astype(F32) + fin_in[1, g, r, :].astype(F32) + both
            out_ref[xr, :] = v.astype(BF16)
            return carry

        lax.fori_loop(0, R // STRIP, strip, 0)
    for i in range(12):
        copies = out_far(i)[0] if i < 4 else out_fin(i)[0]
        copies[i % 2].wait_send()


def combine(layer, x, y, w_o, b_o, w_down, b_down):
    qkv, depth = w_o.shape[1:]
    inner = w_down.shape[1]
    head = qkv // 2
    seq = CHIPS * CHUNK
    vmem, hbm = pl.BlockSpec(memory_space=pltpu.VMEM), pl.BlockSpec(memory_space=pltpu.HBM)
    dma = pltpu.SemaphoreType.DMA
    return pl.pallas_call(
        functools.partial(combine_kernel, layer),
        out_shape=jax.ShapeDtypeStruct(x.shape, BF16),
        in_specs=[vmem] * 3 + [hbm] * 3,
        out_specs=vmem,
        scratch_shapes=[
            pltpu.VMEM((qkv, depth), BF16), pltpu.VMEM((inner, depth), BF16), pltpu.VMEM((seq, qkv), BF16), pltpu.VMEM((seq, qkv), BF16),
            pltpu.VMEM((16, SUB, qkv), BF16), pltpu.VMEM((16, SUB, inner), BF16), pltpu.VMEM((2, CHIPS, SUB, CHUNK), F32),
            pltpu.VMEM((2, SUB, head), F32), pltpu.VMEM((SUB, qkv), BF16), pltpu.VMEM((2, SUB, depth), BF16),
            pltpu.VMEM((4, R, depth), BF16), pltpu.VMEM((2, 2, R, depth), BF16), pltpu.VMEM((2, GROUPS, R, depth), BF16),
            pltpu.VMEM((16, R, depth), BF16),
            dma((3 + depth // 1024,)), dma((16,)), dma((16,)), dma((2,)), dma((4,)), dma((12,)), dma((2, 2)), dma((2, GROUPS)),
        ],
        compiler_params=pltpu.CompilerParams(collective_id=2 * layer + 1, has_side_effects=True, vmem_limit_bytes=VMEM_LIMIT),
        cost_estimate=pl.CostEstimate(flops=2 * seq * depth * (qkv + inner), bytes_accessed=60_000_000, transcendentals=seq * seq),
        name=f"combine_{layer}",
    )(x, b_o, b_down, y, w_o, w_down)


def solution(mesh):
    head_spec = P(None, None, "tp", None)
    head_bias_spec = P(None, "tp", None)
    in_specs = (P("dp", "tp", None), P(), P(), head_spec, head_bias_spec, head_spec, head_bias_spec, head_spec, head_bias_spec,
                P(None, "tp", None, None), P(), P(None, None, "tp"), P(None, "tp"), P(None, "tp", None), P())

    def local_program(x_loc, ln_gain, ln_bias, w_q, b_q, w_k, b_k, w_v, b_v, w_o, b_o, w_up, b_up, w_down, b_down):
        tables = [jnp.asarray(t) for t in rotary_constants(x_loc.shape[1] * mesh.shape["tp"])]
        w_o = w_o.reshape(w_o.shape[0], -1, w_o.shape[3])
        hidden = x_loc.reshape(x_loc.shape[1:])
        for layer in range(w_q.shape[0]):
            y = project(layer, hidden, ln_gain, ln_bias, w_q, b_q, w_k, b_k, w_v, b_v, w_up, b_up, tables)
            hidden = combine(layer, hidden, y, w_o, b_o, w_down, b_down)
        return hidden.reshape(x_loc.shape)

    return jax.shard_map(local_program, mesh=mesh, in_specs=in_specs, out_specs=P("dp", "tp", None), check_vma=False)
```

time: 743 us -> 378 us (0.51)
  Pallas kernels: 0 us -> 375 us
  matrix products: 354 us -> 0 us
  waiting for transfers between devices: 267 us -> 0 us
  local copies, waits for them, and re-layouts: 75.1 us -> 3.13 us
  other arithmetic: 27.6 us -> 0 us
  between operations: 13.7 us -> 0.03 us
    pallas_call x0 -> x4, Pallas kernels: none -> 375 us  [the longest x2 196 us: combine(): pl.pallas_call(functools.partial(combine_kernel, layer), out_shape=jax.Sh...]
    dot_general x12 -> x0, matrix products: 315 us -> none  [the longest x2 95.9 us: branch_partials(): jnp.einsum('blf,fd->bld', up_act, w_down, preferred_element_type=jnp.floa...]
    reduce_scatter x2 -> x0, waiting for transfers between devices: 175 us -> none  [local_program(): returned = lax.psum_scatter(part_sum, 'tp', scatter_dimension=1, tiled=True)]
    all_gather x2 -> x0, waiting for transfers between devices: 91.6 us -> none  [local_program(): gathered = lax.all_gather(normed, 'tp', axis=1, tiled=True)]
    unnamed x54 -> x1, local copies, waits for them, and re-layouts: 46.2 us -> 3.13 us
    sub x2 -> x0, matrix products: 39.2 us -> none  [causal_attention(): jax.nn.softmax(jnp.where(causal, scores, -1e+30), axis=-1)]
    slice x3 -> x0, local copies, waits for them, and re-layouts: 25.4 us -> none  [the longest x1 8.47 us: local_program(): w_k[layer]]
    convert_element_type x11 -> x0, other arithmetic: 15 us -> none  [the longest x2 4.76 us: layer_norm(): (centered * lax.rsqrt(variance + LN_EPS) * gain.astype(jnp.float32) + bia...]
  transfers between devices with their start and end apart: 4 -> 0, of which waited for: 4 -> 0; matrix products, arithmetic and copies ran while one was open for 11% -> 0% of each run, Pallas kernels for 0% -> 0%
where the time goes in v1:
time: 378 us
  Pallas kernels  375 us (99%)
    pallas_call x2, Pallas kernels, combine(): pl.pallas_call(functools.partial(combine_kernel, layer), out_shape=jax.Sh...  196 us
    pallas_call x2, Pallas kernels, project(): pl.pallas_call(functools.partial(project_kernel, layer), out_shape=jax.Sh...  179 us

profile of v1, /device:TPU:81, one launch (start us, length us, event | category | flops | bytes accessed | tf_op | source)
XLA Modules:
  0.0 378.0 jit_solution(10595494086466298597)
XLA Ops:
  0.0 90.9 %project_0.1.y_hbm = bf16[2048,3584]{1,0:T(8,128)(2,1)} custom-call(bf16[256,4096]{1,0:T(8,128)(2,1)} %bitcast.6, bf16[2,4096]{1,0:T(2,128)(2,1)} %gain_ref.3, bf16[2,4096]{1,0:T(2,128)(2,1)} %bias_ref.3, bf16[2,2,256]{2,1,0:T(2,128)(2,1)} %bq_ref.3, bf16[2,2,256]{2,1,0:T(2,128)(2,1)} %bk_ref.3, bf16[2,2,256]{2,1,0:T(2,128)(2,1)} %bv_ref.3, ...), custom_call_target="tpu_custom_call" | custom-call | flops 60129542144 | bytes 60000000 | tf_op jit(solution)/shard_map/project_0/pallas_call | solution.py:245
  90.9 98.0 %combine_0.1.x_ref = bf16[256,4096]{1,0:T(8,128)(2,1)} custom-call(bf16[256,4096]{1,0:T(8,128)(2,1)} %bitcast.7, bf16[2,4096]{1,0:T(2,128)(2,1)} %bo_ref.3, bf16[2,4096]{1,0:T(2,128)(2,1)} %bd_ref.3, bf16[2048,3584]{1,0:T(8,128)(2,1)} %project_0.1.y_hbm, bf16[2,512,4096]{2,1,0:T(8,128)(2,1)} %bitcast.4, bf16[2,2048,4096]{2,1,0:T(8,128)(2,1)} %wd_hbm.3), custom_call_target="tpu_custom_call" | custom-call | flops 42949672960 | bytes 60000000 | tf_op jit(solution)/shard_map/combine_0/pallas_call | solution.py:490
  188.9 87.9 %project_1.1.y_hbm = bf16[2048,3584]{1,0:T(8,128)(2,1)} custom-call(bf16[256,4096]{1,0:T(8,128)(2,1)} %combine_0.1.x_ref, bf16[2,4096]{1,0:T(2,128)(2,1)} %gain_ref.3, bf16[2,4096]{1,0:T(2,128)(2,1)} %bias_ref.3, bf16[2,2,256]{2,1,0:T(2,128)(2,1)} %bq_ref.3, bf16[2,2,256]{2,1,0:T(2,128)(2,1)} %bk_ref.3, bf16[2,2,256]{2,1,0:T(2,128)(2,1)} %bv_ref.3, ...), custom_call_target="tpu_custom_call" | custom-call | flops 60129542144 | bytes 60000000 | tf_op jit(solution)/shard_map/project_1/pallas_call | solution.py:245
  276.8 98.1 %combine_1.1 = bf16[256,4096]{1,0:T(8,128)(2,1)} custom-call(bf16[256,4096]{1,0:T(8,128)(2,1)} %combine_0.1.x_ref, bf16[2,4096]{1,0:T(2,128)(2,1)} %bo_ref.3, bf16[2,4096]{1,0:T(2,128)(2,1)} %bd_ref.3, bf16[2048,3584]{1,0:T(8,128)(2,1)} %project_1.1.y_hbm, bf16[2,512,4096]{2,1,0:T(8,128)(2,1)} %bitcast.5, bf16[2,2048,4096]{2,1,0:T(8,128)(2,1)} %wd_hbm.3), custom_call_target="tpu_custom_call" | custom-call | flops 42949672960 | bytes 60000000 | tf_op jit(solution)/shard_map/combine_1/pallas_call | solution.py:490
  374.9 3.1 copy.21
